TPU v7x, 8 devices: a whole 2x2x1 slice. The times are simulated.
8 devices in a mesh: dp: 1 (over z), tp: 8 (over y, x, core).
Axes of the slice: x: 2, y: 2, z: 1, core: 2. Of those that a mesh axis runs over, the one named last changes fastest.
Arguments:
- hidden: bfloat16 [512, 1024], P('dp')
- positions: int32 [512], P('dp')
- ln1_gain: float32 [2, 1024], replicated
- ln1_bias: float32 [2, 1024], replicated
- ln2_gain: float32 [2, 1024], replicated
- ln2_bias: float32 [2, 1024], replicated
- w_qkv: bfloat16 [2, 1024, 3072], P(None, None, 'tp')
- b_qkv: bfloat16 [2, 3072], P(None, 'tp')
- w_out: bfloat16 [2, 1024, 1024], P(None, 'tp')
- b_out: bfloat16 [2, 1024], replicated
- w_up: bfloat16 [2, 1024, 4096], P(None, None, 'tp')
- b_up: bfloat16 [2, 4096], P(None, 'tp')
- w_down: bfloat16 [2, 4096, 1024], P(None, 'tp')
- b_down: bfloat16 [2, 1024], replicated
- k_cache: bfloat16 [2, 512, 16, 128, 64], P(None, 'dp', 'tp')
- v_cache: bfloat16 [2, 512, 16, 128, 64], P(None, 'dp', 'tp')
Outputs:
- output 1: bfloat16 [512, 1024], P('dp')
- output 2: bfloat16 [2, 512, 16, 128, 64], P(None, 'dp', 'tp')
- output 3: bfloat16 [2, 512, 16, 128, 64], P(None, 'dp', 'tp')
All inputs are finite; a program needn't handle non-finite values.
Results may differ from a plain program's by a relative error of at most 0.0118106.
Values are sent between devices in bfloat16 or wider.
A program may use at most 1 GiB of HBM per device.

v0:
```python
import jax
import jax.numpy as jnp
from jax import lax
from jax.sharding import PartitionSpec as P

EPS = 1e-5


def layer_norm(hid_f32, gain, bias):
    mean_val = jnp.mean(hid_f32, axis=-1, keepdims=True)
    centered = hid_f32 - mean_val
    variance = jnp.mean(centered * centered, axis=-1, keepdims=True)
    return (centered * lax.rsqrt(variance + EPS) * gain + bias).astype(jnp.bfloat16)


def rotate(vecs, positions):
    head_dim = vecs.shape[-1]
    rot_dims = head_dim // 4
    half_dims = head_dim // 8
    inv_freq = 10000.0 ** (-2.0 * jnp.arange(half_dims, dtype=jnp.float32) / rot_dims)
    angle = positions.astype(jnp.float32)[:, None, None] * inv_freq
    cos_a = jnp.cos(angle)
    sin_a = jnp.sin(angle)
    first = vecs[..., :half_dims]
    second = vecs[..., half_dims:rot_dims]
    return jnp.concatenate([first * cos_a - second * sin_a, second * cos_a + first * sin_a, vecs[..., rot_dims:]], axis=-1)


def project(attn_in, w_qkv, b_qkv, positions, num_heads, head_dim):
    qkv_proj = (jnp.dot(attn_in, w_qkv, preferred_element_type=jnp.float32) + b_qkv.astype(jnp.float32)).astype(jnp.bfloat16)
    qkv_proj = qkv_proj.reshape(attn_in.shape[0], num_heads, 3, head_dim)
    query = rotate(qkv_proj[:, :, 0].astype(jnp.float32), positions).astype(jnp.bfloat16)
    key_new = rotate(qkv_proj[:, :, 1].astype(jnp.float32), positions).astype(jnp.bfloat16)
    return query, key_new, qkv_proj[:, :, 2]


def attend(query, key_new, value_new, k_layer, v_layer, positions):
    scale = query.shape[-1] ** -0.5
    old_scores = jnp.einsum('bhd,bhsd->bhs', query, k_layer, preferred_element_type=jnp.float32) * scale
    earlier = jnp.arange(k_layer.shape[2])[None, None, :] < positions[:, None, None]
    old_scores = jnp.where(earlier, old_scores, -1e30)
    cur_score = jnp.einsum('bhd,bhd->bh', query, key_new, preferred_element_type=jnp.float32) * scale
    top_score = jnp.maximum(jnp.max(old_scores, axis=-1), cur_score)
    old_exp = jnp.exp(old_scores - top_score[..., None])
    cur_exp = jnp.exp(cur_score - top_score)
    denom = jnp.sum(old_exp, axis=-1) + cur_exp
    old_prob = (old_exp / denom[..., None]).astype(jnp.bfloat16)
    cur_prob = (cur_exp / denom).astype(jnp.bfloat16)
    context = jnp.einsum('bhs,bhsd->bhd', old_prob, v_layer, preferred_element_type=jnp.float32)
    context = context + cur_prob.astype(jnp.float32)[..., None] * value_new.astype(jnp.float32)
    return context.astype(jnp.bfloat16)


def mlp_branch(mlp_in, w_up, b_up, w_down):
    up_proj = jnp.dot(mlp_in, w_up, preferred_element_type=jnp.float32) + b_up.astype(jnp.float32)
    gelu_out = jax.nn.gelu(up_proj, approximate=False).astype(jnp.bfloat16)
    return jnp.dot(gelu_out, w_down, preferred_element_type=jnp.float32)


def write_slots(cache, new_rows, positions):
    slot_hit = jnp.arange(cache.shape[3])[None, :] == positions[:, None]
    return jnp.where(slot_hit[None, :, None, :, None], new_rows[:, :, :, None, :], cache)


def solution(mesh):
    cache_spec = P(None, 'dp', 'tp', None, None)
    rep_spec = P(None, None)
    in_specs = (P('dp', None), P('dp'), rep_spec, rep_spec, rep_spec, rep_spec,
                P(None, None, 'tp'), P(None, 'tp'), P(None, 'tp', None), rep_spec,
                P(None, None, 'tp'), P(None, 'tp'), P(None, 'tp', None), rep_spec,
                cache_spec, cache_spec)
    out_specs = (P('dp', None), cache_spec, cache_spec)

    def local(hidden, positions, ln1_gain, ln1_bias, ln2_gain, ln2_bias, w_qkv, b_qkv, w_out, b_out, w_up, b_up, w_down, b_down, k_cache, v_cache):
        num_layers, num_rows, heads_local, slots, head_dim = k_cache.shape
        key_list = []
        value_list = []
        for layer in range(num_layers):
            hid_f32 = hidden.astype(jnp.float32)
            attn_in = layer_norm(hid_f32, ln1_gain[layer], ln1_bias[layer])
            mlp_in = layer_norm(hid_f32, ln2_gain[layer], ln2_bias[layer])
            query, key_new, value_new = project(attn_in, w_qkv[layer], b_qkv[layer], positions, heads_local, head_dim)
            context = attend(query, key_new, value_new, k_cache[layer], v_cache[layer], positions)
            attn_part = jnp.dot(context.reshape(num_rows, heads_local * head_dim), w_out[layer], preferred_element_type=jnp.float32)
            attn_sum = lax.psum(attn_part.astype(jnp.bfloat16), 'tp')
            mlp_part = mlp_branch(mlp_in, w_up[layer], b_up[layer], w_down[layer])
            mlp_sum = lax.psum(mlp_part.astype(jnp.bfloat16), 'tp')
            total = hid_f32 + attn_sum.astype(jnp.float32) + mlp_sum.astype(jnp.float32) + b_out[layer].astype(jnp.float32) + b_down[layer].astype(jnp.float32)
            hidden = total.astype(jnp.bfloat16)
            key_list.append(key_new)
            value_list.append(value_new)
        k_out = write_slots(k_cache, jnp.stack(key_list), positions)
        v_out = write_slots(v_cache, jnp.stack(value_list), positions)
        return hidden, k_out, v_out

    return jax.shard_map(local, mesh=mesh, in_specs=in_specs, out_specs=out_specs, check_vma=False)
```

profile of v0, /device:TPU:0, one launch (start us, length us, event | category | flops | bytes accessed | tf_op | source)
XLA Modules:
  0.0 194.3 jit_solution(15169940400799549441)
XLA Ops:
  7.2 0.0 copy-start
  7.2 0.0 all-reduce.7.cloned.1.call-start
  7.3 0.8 convert_element_type.165
  8.1 0.8 iota_compare_fusion
  8.9 1.4 convert_reduce_fusion.1
  10.3 1.6 fusion.29
  12.0 0.6 slice_convert_fusion.6
  12.7 0.6 fusion.263
  13.3 0.6 fusion.264
  13.9 2.0 %fusion.38 = bf16[512,384]{0,1:T(8,128)(2,1)S(1)} fusion(bf16[512,1024]{1,0:T(8,128)(2,1)S(1)} %copy-done, f32[1024]{0:T(1024)S(1)} %bitcast.168, f32[1024]{0:T(1024)S(1)} %bitcast.167, f32[512]{0:T(512)S(1)} %add_rsqrt_fusion.1, f32[512]{0:T(512)S(1)} %broadcast_multiply_fusion.1, bf16[2,1024,384]{2,1,0:T(8,128)(2,1)} %param.22, f32[384]{0:T(512)S(1)} %get-tuple-element.4), kind=kOutput, calls=%fused_computation.56 | convolution fusion | flops 406192128 | bytes 2242048 | tf_op jit(solution)/shard_map/dot_general | solution.py:30
  15.8 0.1 slice_bitcast_fusion.5
  15.9 0.1 multiply_cosine_fusion
  16.1 0.4 copy.35
  16.5 8.0 %fusion.6 = f32[512,2,1,128]{3,2,1,0:T(1,128)S(1)} fusion(bf16[512,2,64,1]{2,3,1,0:T(2,128)(2,1)S(1)} %copy.35, bf16[2,512,2,128,64]{3,4,2,1,0:T(8,128)(2,1)} %param.30), kind=kOutput, calls=%fused_computation.8 | convolution fusion | flops 16777216 | bytes 17432576 | tf_op jit(solution)/shard_map/bhd,bhsd->bhs/dot_general | solution.py:39
  24.6 0.2 fusion.176
  24.8 0.1 fusion.185
  24.9 0.4 fusion.174
  25.3 0.3 fusion.188
  25.7 12.3 %fusion.4 = f32[512,2,1,64]{3,2,1,0:T(1,128)S(1)} fusion(bf16[2,512,2,128,64]{3,4,2,1,0:T(8,128)(2,1)} %param.31, bf16[512,2,128,1]{2,0,1,3:T(8,128)(2,1)S(1)} %fusion.188), kind=kOutput, calls=%fused_computation.6 | convolution fusion | flops 16777216 | bytes 17301504 | tf_op jit(solution)/shard_map/bhs,bhsd->bhd/dot_general | solution.py:49
  37.9 0.7 copy.41
  38.7 1.4 convolution_convert_fusion.1
  40.1 6.0 %convolution_convert_fusion.3 = bf16[512,1024]{1,0:T(8,128)(2,1)} fusion(bf16[2,512,1024]{2,1,0:T(8,128)(2,1)} %param.28, bf16[2,1024,512]{2,1,0:T(8,128)(2,1)} %param.26, bf16[512,1024]{1,0:T(8,128)(2,1)S(1)} %copy-done, f32[1024]{0:T(1024)S(1)} %bitcast.166, f32[1024]{0:T(1024)S(1)} %bitcast.165, f32[512]{0:T(512)S(1)} %add_rsqrt_fusion.1, ...), kind=kOutput, calls=%fused_computation.51 | convolution fusion | flops 1094713344 | bytes 4208640 | tf_op jit(solution)/shard_map/dot_general | solution.py:57
  46.0 0.0 all-reduce.7.cloned.1.call-update
  46.1 0.2 all-reduce.5.cloned.1.call-start
  46.3 0.4 copy-done.2
  46.7 0.0 copy-done.3
  46.8 52.4 %all-reduce.7.cloned.1.call-done = (bf16[512,1024]{1,0:T(8,128)(2,1)}, bf16[512,1024]{1,0:T(8,128)(2,1)}) async-done(((bf16[512,1024]{1,0:T(8,128)(2,1)}, bf16[512,1024]{1,0:T(8,128)(2,1)}), (bf16[512,1024]{1,0:T(8,128)(2,1)}, bf16[512,1024]{1,0:T(8,128)(2,1)})) %all-reduce.7.cloned.1.call-update) | async-done | bytes 2097168 | tf_op jit(solution)/shard_map/psum | solution.py:87
  99.2 2.3 %convert_reduce_fusion = (f32[512]{0:T(512)S(1)}, bf16[512,1024]{1,0:T(8,128)(2,1)S(1)}) fusion(f32[1024]{0:T(1024)S(1)} %bitcast.160, f32[1024]{0:T(1024)S(1)} %bitcast.159, bf16[512,1024]{1,0:T(8,128)(2,1)} %get-tuple-element.7, bf16[512,1024]{1,0:T(8,128)(2,1)} %get-tuple-element.8, bf16[512,1024]{1,0:T(8,128)(2,1)S(1)} %copy-done), kind=kLoop, calls=%fused_computation.16 | loop fusion | flops 5242368 | bytes 4204544 | tf_op jit(solution)/shard_map/reduce_sum | solution.py:10
  101.5 0.4 fusion.28
  102.0 0.9 fusion.39
  102.8 0.1 slice_bitcast_fusion.4
  103.0 0.1 fusion.183
  103.1 0.4 copy.33
  103.5 0.4 copy.34
  103.9 0.4 copy.42
  104.3 8.0 %fusion.2 = f32[512,2,1,128]{3,2,1,0:T(1,128)S(1)} fusion(bf16[512,2,64,1]{2,3,1,0:T(2,128)(2,1)S(1)} %copy.42, bf16[2,512,2,128,64]{3,4,2,1,0:T(8,128)(2,1)} %param.30), kind=kOutput, calls=%fused_computation.4 | convolution fusion | flops 16777216 | bytes 17432576 | tf_op jit(solution)/shard_map/bhd,bhsd->bhs/dot_general | solution.py:39
  112.4 0.2 fusion.177
  112.6 0.4 fusion.175
  113.0 0.3 fusion.189
  113.4 12.2 %fusion = f32[512,2,1,64]{3,2,1,0:T(1,128)S(1)} fusion(bf16[2,512,2,128,64]{3,4,2,1,0:T(8,128)(2,1)} %param.31, bf16[512,2,128,1]{2,0,1,3:T(8,128)(2,1)S(1)} %fusion.189), kind=kOutput, calls=%fused_computation.2 | convolution fusion | flops 16777216 | bytes 17301504 | tf_op jit(solution)/shard_map/bhs,bhsd->bhd/dot_general | solution.py:49
  125.6 0.0 copy-start.14
  125.7 0.6 copy.48
  126.3 2.4 %convolution_convert_fusion = bf16[512,1024]{1,0:T(8,128)(2,1)} fusion(bf16[512,128]{0,1:T(8,128)(2,1)S(1)} %bitcast.152, bf16[2,128,1024]{2,1,0:T(8,128)(2,1)} %param.24), kind=kOutput, calls=%fused_computation.48 | convolution fusion | flops 134742016 | bytes 1441792 | tf_op jit(solution)/shard_map/dot_general | solution.py:84
  128.8 6.0 %convolution_convert_fusion.2 = bf16[512,1024]{1,0:T(8,128)(2,1)} fusion(bf16[2,512,1024]{2,1,0:T(8,128)(2,1)} %param.28, bf16[2,1024,512]{2,1,0:T(8,128)(2,1)} %param.26, bf16[512,1024]{1,0:T(8,128)(2,1)S(1)} %get-tuple-element.10, f32[1024]{0:T(1024)S(1)} %bitcast.162, f32[1024]{0:T(1024)S(1)} %bitcast.161, f32[512]{0:T(512)S(1)} %copy-done.13, ...), kind=kOutput, calls=%fused_computation.50 | convolution fusion | flops 1094713344 | bytes 4208640 | tf_op jit(solution)/shard_map/dot_general | solution.py:57
  134.7 0.0 all-reduce.5.cloned.1.call-update
  134.7 43.9 %broadcast_select_fusion = (bf16[2,512,2,128,64]{3,4,2,1,0:T(8,128)(2,1)}, bf16[2,512,2,128,64]{3,4,2,1,0:T(8,128)(2,1)}) fusion(bf16[2,512,2,128,64]{3,4,2,1,0:T(8,128)(2,1)} %param.31, pred[512,128]{1,0:T(8,128)(4,1)S(1)} %get-tuple-element.51, bf16[2,512,2,64]{3,2,1,0:T(2,128)(2,1)S(1)} %copy.34, bf16[2,512,2,128,64]{3,4,2,1,0:T(8,128)(2,1)} %param.30, ...), kind=kLoop, calls=%fused_computation | loop fusion | flops 33554432 | bytes 134807552 | tf_op jit(solution)/shard_map/jit(_where)/select_n | solution.py:62
  178.6 5.6 %all-reduce.5.cloned.1.call-done = (bf16[512,1024]{1,0:T(8,128)(2,1)}, bf16[512,1024]{1,0:T(8,128)(2,1)}) async-done(((bf16[512,1024]{1,0:T(8,128)(2,1)}, bf16[512,1024]{1,0:T(8,128)(2,1)}), (bf16[512,1024]{1,0:T(8,128)(2,1)}, bf16[512,1024]{1,0:T(8,128)(2,1)})) %all-reduce.5.cloned.1.call-update) | async-done | bytes 2097168 | tf_op jit(solution)/shard_map/psum | solution.py:87
  184.3 3.2 %fusion.37 = bf16[512,1024]{1,0:T(8,128)(2,1)} fusion(bf16[512,1024]{1,0:T(8,128)(2,1)S(1)} %get-tuple-element.10, bf16[512,1024]{1,0:T(8,128)(2,1)} %get-tuple-element.5, bf16[512,1024]{1,0:T(8,128)(2,1)} %get-tuple-element.6, f32[1024]{0:T(1024)S(1)} %bitcast.158, f32[1024]{0:T(1024)S(1)} %bitcast.157), kind=kLoop, calls=%fused_computation.45 | loop fusion | flops 4194304 | bytes 4202496 | tf_op jit(solution)/shard_map/convert_element_type | solution.py:89
  (56 shorter events, 0.5 us)
Async XLA Ops:
  7.2 6.7 %copy-start = (bf16[512,1024]{1,0:T(8,128)(2,1)S(1)}, bf16[512,1024]{1,0:T(8,128)(2,1)}, u32[]{:S(2)}) copy-start(bf16[512,1024]{1,0:T(8,128)(2,1)} %param.16) | copy-start | bytes 3145732
  7.2 4.8 %copy-start.9 = (bf16[2,384]{1,0:T(2,128)(2,1)S(1)}, bf16[2,384]{1,0:T(2,128)(2,1)}, u32[]{:S(2)}) copy-start(bf16[2,384]{1,0:T(2,128)(2,1)} %param.23) | copy-start | bytes 4612
  7.2 4.8 %copy-start.8 = (bf16[2,512]{1,0:T(2,128)(2,1)S(1)}, bf16[2,512]{1,0:T(2,128)(2,1)}, u32[]{:S(2)}) copy-start(bf16[2,512]{1,0:T(2,128)(2,1)} %param.27) | copy-start | bytes 6148
  7.2 5.4 %copy-start.4 = (f32[2,1024]{1,0:T(2,128)S(1)}, f32[2,1024]{1,0:T(2,128)}, u32[]{:S(2)}) copy-start(f32[2,1024]{1,0:T(2,128)} %param.18) | copy-start | bytes 24580
  7.2 5.4 %copy-start.5 = (f32[2,1024]{1,0:T(2,128)S(1)}, f32[2,1024]{1,0:T(2,128)}, u32[]{:S(2)}) copy-start(f32[2,1024]{1,0:T(2,128)} %param.19) | copy-start | bytes 24580
  7.2 5.4 %copy-start.6 = (f32[2,1024]{1,0:T(2,128)S(1)}, f32[2,1024]{1,0:T(2,128)}, u32[]{:S(2)}) copy-start(f32[2,1024]{1,0:T(2,128)} %param.20) | copy-start | bytes 24580
  7.2 6.0 %copy-start.7 = (f32[2,1024]{1,0:T(2,128)S(1)}, f32[2,1024]{1,0:T(2,128)}, u32[]{:S(2)}) copy-start(f32[2,1024]{1,0:T(2,128)} %param.21) | copy-start | bytes 24580
  7.2 92.0 %all-reduce.7.cloned.1.call-start = ((), (), s32[]{:S(2)}) async-start(), calls=%async_computation.1 | async-start | bytes 4194304 | tf_op jit(solution)/shard_map/psum | solution.py:87
  25.6 13.0 %copy-start.1 = (bf16[2,128,1024]{2,1,0:T(8,128)(2,1)S(1)}, bf16[2,128,1024]{2,1,0:T(8,128)(2,1)}, u32[]{:S(2)}) copy-start(bf16[2,128,1024]{2,1,0:T(8,128)(2,1)} %param.24) | copy-start | bytes 1572868
  46.0 0.7 copy-start.2
  46.0 0.7 copy-start.3
  46.1 138.2 %all-reduce.5.cloned.1.call-start = ((), (), s32[]{:S(2)}) async-start(), calls=%async_computation | async-start | bytes 4194304 | tf_op jit(solution)/shard_map/psum | solution.py:87
  99.2 2.8 %copy-start.15 = (bf16[2,1024,384]{2,1,0:T(8,128)(2,1)S(1)}, bf16[2,1024,384]{2,1,0:T(8,128)(2,1)}, u32[]{:S(2)}) copy-start(bf16[2,1024,384]{2,1,0:T(8,128)(2,1)} %param.22) | copy-start | bytes 4718596
  101.9 0.9 copy-start.12
  125.6 3.1 %copy-start.10 = (f32[1,1024]{1,0:T(1,128)S(1)}, f32[1,1024]{1,0:T(1,128)}, u32[]{:S(2)}) copy-start(f32[1,1024]{1,0:T(1,128)} %get-tuple-element.41) | copy-start | bytes 12292
  125.6 3.1 %copy-start.11 = (f32[1,1024]{1,0:T(1,128)S(1)}, f32[1,1024]{1,0:T(1,128)}, u32[]{:S(2)}) copy-start(f32[1,1024]{1,0:T(1,128)} %get-tuple-element.43) | copy-start | bytes 12292
  125.6 3.1 %copy-start.13 = (f32[512]{0:T(512)S(1)}, f32[512]{0:T(512)}, u32[]{:S(2)}) copy-start(f32[512]{0:T(512)} %copy-done.12) | copy-start | bytes 6148
  125.6 3.1 %copy-start.14 = (f32[1,512]{1,0:T(1,128)S(1)}, f32[1,512]{1,0:T(1,128)}, u32[]{:S(2)}) copy-start(f32[1,512]{1,0:T(1,128)} %get-tuple-element.53) | copy-start | bytes 6148
Sparse Core Ops, SparseCore 0:
  46.2 52.9 all-reduce.6
  134.9 49.3 all-reduce.4
where the time goes:
time: 195 us; the launch traced here: 194 us
  matrix products  59.2 us (30%)
  waiting for transfers between devices  58.1 us (30%)
  other arithmetic  57.7 us (30%)
  between operations  14.5 us (7%)
  local copies, waits for them, and re-layouts  4.67 us (2%)
    psum x2, waiting for transfers between devices, local(): mlp_sum = lax.psum(mlp_part.astype(jnp.bfloat16), 'tp')  58 us
    select_n x1, other arithmetic, write_slots(): jnp.where(slot_hit[None, :, None, :, None], new_rows[:, :, :, None, :], c...  43.9 us
    dot_general x2, matrix products, attend(): jnp.einsum('bhs,bhsd->bhd', old_prob, v_layer, preferred_element_type=jnp...  24.5 us
    dot_general x2, matrix products, attend(): jnp.einsum('bhd,bhsd->bhs', query, k_layer, preferred_element_type=jnp.fl...  16.1 us
    dot_general x2, matrix products, mlp_branch(): return jnp.dot(gelu_out, w_down, preferred_element_type=jnp.float32)  11.9 us
  transfers between devices with their start and end apart: 2, of which 2 were waited for; matrix products, arithmetic and copies ran while one was open for 23% of the time, Pallas kernels for 0%

commit v1 on v0

v1 whole, which is shorter than its diff:
```python
import functools

import jax
import jax.numpy as jnp
import numpy as np
from jax import lax
from jax.experimental import pallas as pl
from jax.experimental.pallas import tpu as pltpu
from jax.sharding import PartitionSpec as P

EPS = 1e-5
BF = jnp.bfloat16
F32 = jnp.float32
MESH = pl.DeviceIdType.MESH
LANES = 128
BLOCK = 32
SLOTS = 8
AHEAD = 5
CHUNK = 128


def iota(shape, dim):
    return lax.broadcasted_iota(jnp.int32, shape, dim)


def normalize(hid):
    mean_val = jnp.mean(hid, axis=-1, keepdims=True)
    centered = hid - mean_val
    variance = jnp.mean(centered * centered, axis=-1, keepdims=True)
    return centered * lax.rsqrt(variance + EPS)


def rotary_tables(pos_row, head):
    pos = jnp.transpose(jnp.broadcast_to(pos_row.astype(F32), (CHUNK, LANES)))
    dim = iota((CHUNK, LANES), 1) % head
    half = head // 8
    freq = np.float64(10000.0) ** (-2.0 * np.arange(half) / (2 * half))
    which = dim % half
    inv = jnp.full((CHUNK, LANES), np.float32(freq[0]), F32)
    for i in range(1, half):
        inv = jnp.where(which == i, np.float32(freq[i]), inv)
    angle = pos * inv
    cos_a = jnp.cos(angle)
    sin_a = jnp.sin(angle)
    cos_t = jnp.where(dim < 2 * half, cos_a, 1.0)
    sin_lo = jnp.where(dim < half, -sin_a, 0.0)
    sin_hi = jnp.where((dim >= half) & (dim < 2 * half), sin_a, 0.0)
    return pos, cos_t, sin_lo, sin_hi


def rotate(x, tables, half):
    cos_t, sin_lo, sin_hi = tables
    up = pltpu.roll(x, LANES - half, 1)
    down = pltpu.roll(x, half, 1)
    return x * cos_t + up * sin_lo + down * sin_hi


def attend_kernel(layer, num_rows, head, *refs):
    (pos_ref, hid_any, gain_ref, bias_ref, w_any, b_ref, k_in, v_in) = refs[:8]
    refs = refs[8:]
    if layer > 0:
        refs = refs[2:]
    (k_out, v_out, ctx_ref, hid_s, w_s, q_s, pos_s, kn_s, vn_s, k_buf, v_buf, rd_sem, wr_sem, in_sem) = refs
    num_blocks = num_rows // BLOCK
    per_chunk = CHUNK // BLOCK

    def reads(blk, slot):
        rows = pl.ds(blk * BLOCK, BLOCK)
        return (pltpu.make_async_copy(k_in.at[layer, rows], k_buf.at[slot], rd_sem.at[0, slot]),
                pltpu.make_async_copy(v_in.at[layer, rows], v_buf.at[slot], rd_sem.at[1, slot]))

    def writes(blk, slot):
        rows = pl.ds(blk * BLOCK, BLOCK)
        return (pltpu.make_async_copy(k_buf.at[slot], k_out.at[layer, rows], wr_sem.at[0, slot]),
                pltpu.make_async_copy(v_buf.at[slot], v_out.at[layer, rows], wr_sem.at[1, slot]))

    hid_copy = pltpu.make_async_copy(hid_any, hid_s, in_sem.at[0])
    w_copy = pltpu.make_async_copy(w_any.at[layer], w_s, in_sem.at[1])
    hid_copy.start()
    w_copy.start()
    for blk in range(SLOTS):
        for copy in reads(blk, blk):
            copy.start()
    hid_copy.wait()
    w_copy.wait()

    lane = iota((CHUNK, LANES), 1)
    low = lane < head

    @pl.loop(0, num_rows // CHUNK)
    def _(c):
        rows = pl.ds(pl.multiple_of(c * CHUNK, CHUNK), CHUNK)
        pos, *tables = rotary_tables(pos_ref[pl.ds(c, 1), :], head)
        pos_s[rows, :] = pos
        normed = normalize(hid_s[rows, :].astype(F32))
        attn_in = (normed * gain_ref[layer:layer + 1, :] + bias_ref[layer:layer + 1, :]).astype(BF)
        qkv = jnp.dot(attn_in, w_s[...], preferred_element_type=F32) + b_ref[layer:layer + 1, :].astype(F32)
        qkv = qkv.astype(BF).astype(F32)
        one, two, three = qkv[:, :LANES], qkv[:, LANES:2 * LANES], qkv[:, 2 * LANES:]
        query = jnp.where(low, one, two)
        key = pltpu.roll(jnp.where(low, three, one), head, 1)
        value = jnp.where(low, two, three)
        q_s[rows, :] = rotate(query, tables, head // 8).astype(BF).astype(F32)
        key_t = jnp.transpose(rotate(key, tables, head // 8).astype(BF).astype(F32))
        val_t = jnp.transpose(value)
        for i in range(per_chunk):
            kn_s[c * per_chunk + i] = (pltpu.roll(key_t, (LANES - i * BLOCK) % LANES, 1) if i else key_t).astype(kn_s.dtype)
            vn_s[c * per_chunk + i] = (pltpu.roll(val_t, (LANES - i * BLOCK) % LANES, 1) if i else val_t).astype(vn_s.dtype)

    scale = head ** -0.5
    sub16 = iota((16, LANES), 0) % 8
    lane16 = iota((16, LANES), 1)
    lane8 = iota((8, LANES), 1)
    even = (sub16 % 2) == 0
    first = sub16 < 4
    upper = (sub16 % 4) < 2

    def merged(buf, new_s, slot, blk, j, hit):
        col = jnp.broadcast_to(new_s[blk][:, j:j + 1], (LANES, LANES)).astype(BF)
        out = jnp.where(hit, col, buf[slot, j])
        buf[slot, j] = out
        return out

    def square(tiles):
        return jnp.concatenate([jnp.concatenate(tiles[:2], 1), jnp.concatenate(tiles[2:], 1)], 0)

    @pl.loop(0, num_blocks)
    def _(blk):
        slot = lax.rem(blk, SLOTS)

        @pl.when((blk + AHEAD >= SLOTS) & (blk + AHEAD < num_blocks))
        def _():
            ahead = blk + AHEAD
            ahead_slot = lax.rem(ahead, SLOTS)
            for copy in writes(ahead - SLOTS, ahead_slot):
                copy.wait()
            for copy in reads(ahead, ahead_slot):
                copy.start()

        for copy in reads(blk, slot):
            copy.wait()

        base = pl.multiple_of(blk * BLOCK, BLOCK)
        for g in range(BLOCK // 8):
            rows = pl.ds(base + 8 * g, 8)
            q8 = q_s[rows, :]
            p8 = pos_s[rows, :]
            hits = [lane.astype(BF) == jnp.broadcast_to(p8[j:j + 1, :], (LANES, LANES)).astype(BF) for j in range(8)]
            q16 = jnp.concatenate([jnp.where(lane8 < head, q8, 0.0), jnp.where(lane8 < head, 0.0, q8)], 0)
            p16 = jnp.concatenate([p8, p8], 0)
            scores = []
            for t in range(2):
                keys = square([merged(k_buf, kn_s, slot, blk, 8 * g + 4 * t + i, hits[4 * t + i]) for i in range(4)])
                mine = first if t == 0 else ~first
                lhs = jnp.concatenate([jnp.where(mine & upper, q16, 0.0), jnp.where(mine & ~upper, q16, 0.0)], 1).astype(BF)
                out = jnp.dot(lhs, keys, preferred_element_type=F32)
                scores.append(jnp.where(even, out[:, :LANES], out[:, LANES:]))
            s = jnp.where(first, scores[0], scores[1]) * scale
            s = jnp.where(lane16.astype(F32) <= p16, s, -1e30)
            e = jnp.exp(s - jnp.max(s, axis=-1, keepdims=True))
            prob = e / jnp.sum(e, axis=-1, keepdims=True)
            lhs = jnp.concatenate([jnp.where(even, prob, 0.0), jnp.where(even, 0.0, prob)], 1).astype(BF)
            ctx = []
            for t in range(2):
                vals = square([merged(v_buf, vn_s, slot, blk, 8 * g + 4 * t + i, hits[4 * t + i]) for i in range(4)])
                out = lax.dot_general(lhs, vals, (((1,), (1,)), ((), ())), preferred_element_type=F32)
                ctx.append(jnp.where(upper, out[:, :LANES], out[:, LANES:]))
            c16 = jnp.where(first, ctx[0], ctx[1])
            ctx_ref[rows, :] = jnp.where(lane8 < head, c16[:8], c16[8:])

        for copy in writes(blk, slot):
            copy.start()

    for blk in range(num_blocks - SLOTS, num_blocks):
        for copy in writes(blk, blk % SLOTS):
            copy.wait()


def attend(layer, positions, hidden, gain, bias, w_qkv, b_qkv, k_cache, v_cache, prev):
    num_rows, width = hidden.shape
    _, _, inner, slots = k_cache.shape
    head = inner // 2
    num_blocks = num_rows // BLOCK
    vmem = pl.BlockSpec(memory_space=pltpu.VMEM)
    anyspace = pl.BlockSpec(memory_space=pl.ANY)
    operands = [positions, hidden, gain, bias, w_qkv, b_qkv, k_cache, v_cache]
    specs = [vmem, anyspace, vmem, vmem, anyspace, vmem, anyspace, anyspace]
    aliases = {}
    if prev is not None:
        operands += list(prev)
        specs += [anyspace, anyspace]
        aliases = {8: 0, 9: 1}
    cache = jax.ShapeDtypeStruct(k_cache.shape, BF)
    return pl.pallas_call(
        functools.partial(attend_kernel, layer, num_rows, head),
        out_shape=(cache, cache, jax.ShapeDtypeStruct((num_rows, inner), F32)),
        in_specs=specs,
        out_specs=(anyspace, anyspace, vmem),
        scratch_shapes=[
            pltpu.VMEM((num_rows, width), BF),
            pltpu.VMEM(w_qkv.shape[1:], BF),
            pltpu.VMEM((num_rows, LANES), F32),
            pltpu.VMEM((num_rows, LANES), F32),
            pltpu.VMEM((num_blocks, LANES, LANES), F32),
            pltpu.VMEM((num_blocks, LANES, LANES), F32),
            pltpu.VMEM((SLOTS, BLOCK, inner, slots), BF),
            pltpu.VMEM((SLOTS, BLOCK, inner, slots), BF),
            pltpu.SemaphoreType.DMA((2, SLOTS)),
            pltpu.SemaphoreType.DMA((2, SLOTS)),
            pltpu.SemaphoreType.DMA((2,)),
        ],
        input_output_aliases=aliases,
        compiler_params=pltpu.CompilerParams(vmem_limit_bytes=56 * 1024 * 1024),
        name=f"attend{layer}",
    )(*operands)


def combine_kernel(layer, num_rows, hid_ref, ctx_ref, gain_ref, bias_ref, w_out_any, w_up_any, b_up_ref, w_down_any, b_out_ref, b_down_ref,
                   out_ref, w_out, w_up, w_down, part, half, pair_in, quad_in, final, in_sem,
                   pair_send, pair_recv, quad_send, quad_recv, gather_send, gather_recv, fwd_send, fwd_recv):
    me = lax.axis_index("tp")
    core = lax.rem(me, 2)
    chip = lax.div(me, 2)
    partner = me + 1 - 2 * core
    others = []
    for k in range(1, 4):
        x = lax.rem(chip, 2)
        y = lax.div(chip, 2)
        ox = 1 - x if k & 1 else x
        oy = 1 - y if k & 2 else y
        others.append(2 * oy + ox)
    num_chunks = num_rows // CHUNK
    half_rows = CHUNK // 2
    piece = CHUNK // 8

    weights = [pltpu.make_async_copy(src.at[layer], dst, in_sem.at[i])
               for i, (src, dst) in enumerate([(w_up_any, w_up), (w_down_any, w_down), (w_out_any, w_out)])]
    for copy in weights:
        copy.start()

    barrier = pltpu.get_barrier_semaphore()
    peers = [partner] + [2 * o + core for o in others]
    for peer in peers:
        pl.semaphore_signal(barrier, inc=1, device_id={"tp": peer}, device_id_type=MESH)

    def remote(src, dst, send, recv, device):
        return pltpu.make_async_remote_copy(src_ref=src, dst_ref=dst, send_sem=send, recv_sem=recv,
                                            device_id={"tp": device}, device_id_type=MESH)

    def pair_copy(c):
        start = pl.multiple_of((1 - core) * half_rows, half_rows)
        return remote(part.at[c, pl.ds(start, half_rows)], pair_in.at[c], pair_send.at[c], pair_recv.at[c], partner)

    def quad_copy(c, k):
        start = pl.multiple_of(others[k] * piece, piece)
        return remote(half.at[c, pl.ds(start, piece)], quad_in.at[c, k], quad_send.at[c, k], quad_recv.at[c, k], 2 * others[k] + core)

    def piece_rows(c, owner_core, owner_chip):
        return pl.ds(pl.multiple_of(c * CHUNK + owner_core * half_rows + owner_chip * piece, piece), piece)

    def gather_copy(c, k):
        rows = piece_rows(c, core, chip)
        return remote(final.at[rows], final.at[rows], gather_send.at[c, k], gather_recv.at[c, k], 2 * others[k] + core)

    def fwd_copy(c):
        rows = pl.ds(pl.multiple_of(c * CHUNK + core * half_rows, half_rows), half_rows)
        return remote(final.at[rows], final.at[rows], fwd_send.at[c], fwd_recv.at[c], partner)

    def compute(c):
        rows = pl.ds(c * CHUNK, CHUNK)
        normed = normalize(hid_ref[rows, :].astype(F32))
        mlp_in = (normed * gain_ref[layer:layer + 1, :] + bias_ref[layer:layer + 1, :]).astype(BF)
        up = jnp.dot(mlp_in, w_up[...], preferred_element_type=F32) + b_up_ref[layer:layer + 1, :].astype(F32)
        act = (0.5 * up * (1.0 + lax.erf(up * np.float32(np.sqrt(0.5))))).astype(BF)
        total = jnp.dot(act, w_down[...], preferred_element_type=F32)
        total = total + jnp.dot(ctx_ref[rows, :].astype(BF), w_out[...], preferred_element_type=F32)
        part[c] = total.astype(BF)

    def pair_done(c):
        pair_copy(c).wait()
        mine = pl.ds(pl.multiple_of(core * half_rows, half_rows), half_rows)
        half[c] = (part[c, mine, :].astype(F32) + pair_in[c].astype(F32)).astype(BF)

    def quad_done(c):
        for k in range(3):
            quad_copy(c, k).wait()
        mine = pl.ds(pl.multiple_of(chip * piece, piece), piece)
        rows = piece_rows(c, core, chip)
        total = hid_ref[rows, :].astype(F32) + half[c, mine, :].astype(F32)
        for k in range(3):
            total = total + quad_in[c, k].astype(F32)
        total = total + b_out_ref[layer:layer + 1, :].astype(F32) + b_down_ref[layer:layer + 1, :].astype(F32)
        final[rows, :] = total.astype(BF)

    for copy in weights:
        copy.wait()
    for step in range(num_chunks + 4):
        if step < num_chunks:
            compute(step)
            if step == 0:
                pl.semaphore_wait(barrier, len(peers))
            pair_copy(step).start()
        if 0 <= step - 1 < num_chunks:
            pair_done(step - 1)
            for k in range(3):
                quad_copy(step - 1, k).start()
        if 0 <= step - 2 < num_chunks:
            quad_done(step - 2)
            for k in range(3):
                gather_copy(step - 2, k).start()
        if 0 <= step - 3 < num_chunks:
            for k in range(3):
                gather_copy(step - 3, k).wait()
            fwd_copy(step - 3).start()
        if 0 <= step - 4 < num_chunks:
            fwd_copy(step - 4).wait()
            rows = pl.ds((step - 4) * CHUNK, CHUNK)
            out_ref[rows, :] = final[rows, :]


def combine(layer, hidden, ctx, gain, bias, w_out, w_up, b_up, w_down, b_out, b_down):
    num_rows, width = hidden.shape
    num_chunks = num_rows // CHUNK
    vmem = pl.BlockSpec(memory_space=pltpu.VMEM)
    anyspace = pl.BlockSpec(memory_space=pl.ANY)
    dma = pltpu.SemaphoreType.DMA
    return pl.pallas_call(
        functools.partial(combine_kernel, layer, num_rows),
        out_shape=jax.ShapeDtypeStruct((num_rows, width), BF),
        in_specs=[vmem, vmem, vmem, vmem, anyspace, anyspace, vmem, anyspace, vmem, vmem],
        out_specs=vmem,
        scratch_shapes=[
            pltpu.VMEM(w_out.shape[1:], BF),
            pltpu.VMEM(w_up.shape[1:], BF),
            pltpu.VMEM(w_down.shape[1:], BF),
            pltpu.VMEM((num_chunks, CHUNK, width), BF),
            pltpu.VMEM((num_chunks, CHUNK // 2, width), BF),
            pltpu.VMEM((num_chunks, CHUNK // 2, width), BF),
            pltpu.VMEM((num_chunks, 3, CHUNK // 8, width), BF),
            pltpu.VMEM((num_rows, width), BF),
            dma((3,)),
            dma((num_chunks,)), dma((num_chunks,)),
            dma((num_chunks, 3)), dma((num_chunks, 3)),
            dma((num_chunks, 3)), dma((num_chunks, 3)),
            dma((num_chunks,)), dma((num_chunks,)),
        ],
        compiler_params=pltpu.CompilerParams(collective_id=layer, has_side_effects=True, vmem_limit_bytes=48 * 1024 * 1024),
        name=f"combine{layer}",
    )(hidden, ctx, gain, bias, w_out, w_up, b_up, w_down, b_out, b_down)


def solution(mesh):
    cache_spec = P(None, 'dp', 'tp', None, None)
    rep_spec = P(None, None)
    in_specs = (P('dp', None), P('dp'), rep_spec, rep_spec, rep_spec, rep_spec,
                P(None, None, 'tp'), P(None, 'tp'), P(None, 'tp', None), rep_spec,
                P(None, None, 'tp'), P(None, 'tp'), P(None, 'tp', None), rep_spec,
                cache_spec, cache_spec)
    out_specs = (P('dp', None), cache_spec, cache_spec)

    def local(hidden, positions, ln1_gain, ln1_bias, ln2_gain, ln2_bias, w_qkv, b_qkv, w_out, b_out, w_up, b_up, w_down, b_down, k_cache, v_cache):
        num_layers, num_rows, heads_local, slots, head_dim = k_cache.shape
        flat = (num_layers, num_rows, heads_local * head_dim, slots)
        k_flat = jnp.swapaxes(k_cache, 3, 4).reshape(flat)
        v_flat = jnp.swapaxes(v_cache, 3, 4).reshape(flat)
        pos = positions.reshape(num_rows // CHUNK, CHUNK)
        prev = None
        for layer in range(num_layers):
            k_out, v_out, ctx = attend(layer, pos, hidden, ln1_gain, ln1_bias, w_qkv, b_qkv, k_flat, v_flat, prev)
            prev = (k_out, v_out)
            hidden = combine(layer, hidden, ctx, ln2_gain, ln2_bias, w_out, w_up, b_up, w_down, b_out, b_down)
        shape = (num_layers, num_rows, heads_local, head_dim, slots)
        return hidden, jnp.swapaxes(prev[0].reshape(shape), 3, 4), jnp.swapaxes(prev[1].reshape(shape), 3, 4)

    return jax.shard_map(local, mesh=mesh, in_specs=in_specs, out_specs=out_specs, check_vma=False)
```

time: 195 us -> 125 us (0.64)
  Pallas kernels: 0 us -> 119 us
  matrix products: 59.2 us -> 0 us
  waiting for transfers between devices: 58.1 us -> 0 us
  other arithmetic: 57.7 us -> 0 us
  between operations: 14.5 us -> 0.82 us
    pallas_call x0 -> x4, Pallas kernels: none -> 119 us  [the longest x2 74 us: attend(): pl.pallas_call(functools.partial(attend_kernel, layer, num_rows, head), o...]
    dot_general x10 -> x0, matrix products: 59.2 us -> none  [the longest x2 24.5 us: attend(): jnp.einsum('bhs,bhsd->bhd', old_prob, v_layer, preferred_element_type=jnp...]
    psum x2 -> x0, waiting for transfers between devices: 58 us -> none  [local(): mlp_sum = lax.psum(mlp_part.astype(jnp.bfloat16), 'tp')]
    select_n x1 -> x0, other arithmetic: 43.9 us -> none  [write_slots(): jnp.where(slot_hit[None, :, None, :, None], new_rows[:, :, :, None, :], c...]
    reduce_sum x6 -> x0, other arithmetic: 6.55 us -> none  [the longest x2 3.74 us: layer_norm(): mean_val = jnp.mean(hid_f32, axis=-1, keepdims=True)]
    convert_element_type x8 -> x0, other arithmetic: 4.76 us -> none  [the longest x1 3.2 us: local(): hidden = total.astype(jnp.bfloat16)]
    unnamed x32 -> x25, local copies, waits for them, and re-layouts: 0.52 us -> 5.09 us
  transfers between devices with their start and end apart: 2 -> 0, of which waited for: 2 -> 0; matrix products, arithmetic and copies ran while one was open for 23% -> 0% of each run, Pallas kernels for 0% -> 0%
where the time goes in v1:
time: 125 us
  Pallas kernels  119 us (95%)
  local copies, waits for them, and re-layouts  5.09 us (4%)
    pallas_call x2, Pallas kernels, attend(): pl.pallas_call(functools.partial(attend_kernel, layer, num_rows, head), o...  74 us
    pallas_call x2, Pallas kernels, combine(): pl.pallas_call(functools.partial(combine_kernel, layer, num_rows), out_sh...  44.7 us
    unnamed x25, local copies, waits for them, and re-layouts  5.09 us

profile of v1, /device:TPU:0, one launch (start us, length us, event | category | flops | bytes accessed | tf_op | source)
XLA Modules:
  0.0 124.6 jit_solution(14943768331330804511)
XLA Ops:
  0.6 0.0 copy-start.2
  0.6 0.0 copy-start.3
  0.7 0.0 copy-start.4
  0.7 0.0 copy-start.7
  0.7 0.0 copy-start.8
  0.7 0.0 copy-start.9
  0.7 0.0 copy-start.10
  0.7 0.0 copy-start.11
  0.7 37.2 %attend0.1 = (bf16[2,512,128,128]{3,2,1,0:T(8,128)(2,1)}, bf16[2,512,128,128]{3,2,1,0:T(8,128)(2,1)}, f32[512,128]{1,0:T(8,128)}) custom-call(s32[4,128]{1,0:T(4,128)} %bitcast.19, bf16[512,1024]{1,0:T(8,128)(2,1)} %hid_ref.1, f32[2,1024]{1,0:T(2,128)} %refs_2_.3, f32[2,1024]{1,0:T(2,128)} %refs_3_.3, bf16[2,1024,384]{2,1,0:T(8,128)(2,1)} %refs_4_.3, ...), custom_call_target="tpu_custom_call" | custom-call | tf_op jit(solution)/shard_map/attend0/pallas_call | solution.py:194
  37.9 0.0 copy-done.2
  38.0 0.0 copy-done.3
  38.0 0.0 copy-done.4
  38.0 0.0 copy-done.7
  38.0 0.0 copy-done.8
  38.0 0.0 copy-done.9
  38.0 0.0 copy-done.10
  38.0 0.0 copy-done.11
  38.0 0.0 copy-start.6
  38.0 0.9 copy-done.6
  39.0 23.9 %combine0.1.refs_1_.hid_ref = bf16[512,1024]{1,0:T(8,128)(2,1)S(1)} custom-call(bf16[512,1024]{1,0:T(8,128)(2,1)S(1)} %copy-done.3, f32[512,128]{1,0:T(8,128)S(1)} %copy-done.6, f32[2,1024]{1,0:T(2,128)S(1)} %copy-done.7, f32[2,1024]{1,0:T(2,128)S(1)} %copy-done.8, bf16[2,128,1024]{2,1,0:T(8,128)(2,1)S(1)} %copy-done.4, bf16[2,1024,512]{2,1,0:T(8,128)(2,1)S(1)} %copy-done.2, ...), custom_call_target="tpu_custom_call" | custom-call | tf_op jit(solution)/shard_map/combine0/pallas_call | solution.py:327
  62.9 0.0 copy-start
  62.9 1.0 copy-done
  63.8 36.8 %attend1.1 = (bf16[2,512,128,128]{3,2,1,0:T(8,128)(2,1)}, bf16[2,512,128,128]{3,2,1,0:T(8,128)(2,1)}, f32[512,128]{1,0:T(8,128)}) custom-call(s32[4,128]{1,0:T(4,128)} %bitcast.20, bf16[512,1024]{1,0:T(8,128)(2,1)} %copy-done, f32[2,1024]{1,0:T(2,128)} %refs_2_.3, f32[2,1024]{1,0:T(2,128)} %refs_3_.3, ...), custom_call_target="tpu_custom_call", output_to_operand_aliasing={{0}: (8, {}), {1}: (9, {})} | custom-call | tf_op jit(solution)/shard_map/attend1/pallas_call | solution.py:194
  100.7 0.0 copy-start.1
  100.7 1.2 copy-done.1
  101.9 0.0 copy-start.5
  101.9 0.9 copy-done.5
  102.9 20.8 %combine1.1 = bf16[512,1024]{1,0:T(8,128)(2,1)S(1)} custom-call(bf16[512,1024]{1,0:T(8,128)(2,1)S(1)} %copy-done.1, f32[512,128]{1,0:T(8,128)S(1)} %copy-done.5, f32[2,1024]{1,0:T(2,128)S(1)} %copy-done.7, f32[2,1024]{1,0:T(2,128)S(1)} %copy-done.8, bf16[2,128,1024]{2,1,0:T(8,128)(2,1)S(1)} %copy-done.4, bf16[2,1024,512]{2,1,0:T(8,128)(2,1)S(1)} %copy-done.2, ...), custom_call_target="tpu_custom_call" | custom-call | tf_op jit(solution)/shard_map/combine1/pallas_call | solution.py:327
  123.6 1.0 copy.24
Async XLA Ops:
  0.6 37.3 %copy-start.2 = (bf16[2,1024,512]{2,1,0:T(8,128)(2,1)S(1)}, bf16[2,1024,512]{2,1,0:T(8,128)(2,1)}, u32[]{:S(2)}) copy-start(bf16[2,1024,512]{2,1,0:T(8,128)(2,1)} %w_up_any.3) | copy-start | bytes 6291460
  0.6 37.3 %copy-start.3 = (bf16[512,1024]{1,0:T(8,128)(2,1)S(1)}, bf16[512,1024]{1,0:T(8,128)(2,1)}, u32[]{:S(2)}) copy-start(bf16[512,1024]{1,0:T(8,128)(2,1)} %hid_ref.1) | copy-start | bytes 3145732
  0.7 37.3 %copy-start.4 = (bf16[2,128,1024]{2,1,0:T(8,128)(2,1)S(1)}, bf16[2,128,1024]{2,1,0:T(8,128)(2,1)}, u32[]{:S(2)}) copy-start(bf16[2,128,1024]{2,1,0:T(8,128)(2,1)} %w_out_any.3) | copy-start | bytes 1572868
  0.7 37.3 %copy-start.7 = (f32[2,1024]{1,0:T(2,128)S(1)}, f32[2,1024]{1,0:T(2,128)}, u32[]{:S(2)}) copy-start(f32[2,1024]{1,0:T(2,128)} %gain_ref.3) | copy-start | bytes 24580
  0.7 37.3 %copy-start.8 = (f32[2,1024]{1,0:T(2,128)S(1)}, f32[2,1024]{1,0:T(2,128)}, u32[]{:S(2)}) copy-start(f32[2,1024]{1,0:T(2,128)} %bias_ref.3) | copy-start | bytes 24580
  0.7 37.3 %copy-start.9 = (bf16[2,1024]{1,0:T(2,128)(2,1)S(1)}, bf16[2,1024]{1,0:T(2,128)(2,1)}, u32[]{:S(2)}) copy-start(bf16[2,1024]{1,0:T(2,128)(2,1)} %b_out_ref.3) | copy-start | bytes 12292
  0.7 37.3 %copy-start.10 = (bf16[2,1024]{1,0:T(2,128)(2,1)S(1)}, bf16[2,1024]{1,0:T(2,128)(2,1)}, u32[]{:S(2)}) copy-start(bf16[2,1024]{1,0:T(2,128)(2,1)} %b_down_ref.3) | copy-start | bytes 12292
  0.7 37.3 %copy-start.11 = (bf16[2,512]{1,0:T(2,128)(2,1)S(1)}, bf16[2,512]{1,0:T(2,128)(2,1)}, u32[]{:S(2)}) copy-start(bf16[2,512]{1,0:T(2,128)(2,1)} %b_up_ref.3) | copy-start | bytes 6148
  38.0 1.0 copy-start.6
  62.9 1.0 copy-start
  100.7 1.2 copy-start.1
  101.9 0.9 copy-start.5

commit v2 on v1

--- a/solution.py
+++ b/solution.py
@@ -56,8 +56,8 @@
 
 
 def attend_kernel(layer, num_rows, head, *refs):
-    (pos_ref, hid_any, gain_ref, bias_ref, w_any, b_ref, k_in, v_in) = refs[:8]
-    refs = refs[8:]
+    (pos_ref, pos_sm, hid_any, gain_ref, bias_ref, w_any, b_ref, k_in, v_in) = refs[:9]
+    refs = refs[9:]
     if layer > 0:
         refs = refs[2:]
     (k_out, v_out, ctx_ref, hid_s, w_s, q_s, pos_s, kn_s, vn_s, k_buf, v_buf, rd_sem, wr_sem, in_sem) = refs
@@ -116,7 +116,8 @@
     upper = (sub16 % 4) < 2
 
     def merged(buf, new_s, slot, blk, j, hit):
-        col = jnp.broadcast_to(new_s[blk][:, j:j + 1], (LANES, LANES)).astype(BF)
+        shift = lax.rem(pos_sm[blk * BLOCK + j] + (LANES - j), LANES)
+        col = pltpu.roll(new_s[blk], shift, 1).astype(BF)
         out = jnp.where(hit, col, buf[slot, j])
         buf[slot, j] = out
         return out
@@ -183,13 +184,13 @@
     num_blocks = num_rows // BLOCK
     vmem = pl.BlockSpec(memory_space=pltpu.VMEM)
     anyspace = pl.BlockSpec(memory_space=pl.ANY)
-    operands = [positions, hidden, gain, bias, w_qkv, b_qkv, k_cache, v_cache]
-    specs = [vmem, anyspace, vmem, vmem, anyspace, vmem, anyspace, anyspace]
+    operands = [positions, positions.reshape(-1), hidden, gain, bias, w_qkv, b_qkv, k_cache, v_cache]
+    specs = [vmem, pl.BlockSpec(memory_space=pltpu.SMEM), anyspace, vmem, vmem, anyspace, vmem, anyspace, anyspace]
     aliases = {}
     if prev is not None:
         operands += list(prev)
         specs += [anyspace, anyspace]
-        aliases = {8: 0, 9: 1}
+        aliases = {9: 0, 10: 1}
     cache = jax.ShapeDtypeStruct(k_cache.shape, BF)
     return pl.pallas_call(
         functools.partial(attend_kernel, layer, num_rows, head),

time: 125 us -> 125 us (level)
  no operation moved by 1% of the time
where the time goes in v2:
time: 125 us; the launch traced here: 124 us
  Pallas kernels  118 us (94%)
  local copies, waits for them, and re-layouts  5.09 us (4%)
    pallas_call x2, Pallas kernels, attend(): pl.pallas_call(functools.partial(attend_kernel, layer, num_rows, head), o...  73.8 us
    pallas_call x2, Pallas kernels, combine(): pl.pallas_call(functools.partial(combine_kernel, layer, num_rows), out_sh...  44.6 us
    unnamed x25, local copies, waits for them, and re-layouts  5.09 us

profile of v2, /device:TPU:0, one launch (start us, length us, event | category | flops | bytes accessed | tf_op | source)
XLA Modules:
  0.0 124.4 jit_solution(17473714218391659995)
XLA Ops:
  0.6 0.0 copy-start.2
  0.6 0.0 copy-start.3
  0.7 0.0 copy-start.4
  0.7 0.0 copy-start.7
  0.7 0.0 copy-start.8
  0.7 0.0 copy-start.9
  0.7 0.0 copy-start.10
  0.7 0.0 copy-start.11
  0.7 37.1 %attend0.1 = (bf16[2,512,128,128]{3,2,1,0:T(8,128)(2,1)}, bf16[2,512,128,128]{3,2,1,0:T(8,128)(2,1)}, f32[512,128]{1,0:T(8,128)}) custom-call(s32[4,128]{1,0:T(4,128)} %bitcast.19, s32[512]{0:T(512)} %refs_1_.3, bf16[512,1024]{1,0:T(8,128)(2,1)} %hid_ref.1, f32[2,1024]{1,0:T(2,128)} %refs_3_.3, f32[2,1024]{1,0:T(2,128)} %refs_4_.3, ...), custom_call_target="tpu_custom_call" | custom-call | tf_op jit(solution)/shard_map/attend0/pallas_call | solution.py:195
  37.8 0.0 copy-done.2
  37.8 0.0 copy-done.3
  37.9 0.0 copy-done.4
  37.9 0.0 copy-done.7
  37.9 0.0 copy-done.8
  37.9 0.0 copy-done.9
  37.9 0.0 copy-done.10
  37.9 0.0 copy-done.11
  37.9 0.0 copy-start.6
  37.9 0.9 copy-done.6
  38.9 23.9 %combine0.1.refs_2_.hid_ref = bf16[512,1024]{1,0:T(8,128)(2,1)S(1)} custom-call(bf16[512,1024]{1,0:T(8,128)(2,1)S(1)} %copy-done.3, f32[512,128]{1,0:T(8,128)S(1)} %copy-done.6, f32[2,1024]{1,0:T(2,128)S(1)} %copy-done.7, f32[2,1024]{1,0:T(2,128)S(1)} %copy-done.8, bf16[2,128,1024]{2,1,0:T(8,128)(2,1)S(1)} %copy-done.4, bf16[2,1024,512]{2,1,0:T(8,128)(2,1)S(1)} %copy-done.2, ...), custom_call_target="tpu_custom_call" | custom-call | tf_op jit(solution)/shard_map/combine0/pallas_call | solution.py:328
  62.8 0.0 copy-start
  62.8 1.0 copy-done
  63.7 36.7 %attend1.1 = (bf16[2,512,128,128]{3,2,1,0:T(8,128)(2,1)}, bf16[2,512,128,128]{3,2,1,0:T(8,128)(2,1)}, f32[512,128]{1,0:T(8,128)}) custom-call(s32[4,128]{1,0:T(4,128)} %bitcast.20, s32[512]{0:T(512)} %refs_1_.3, bf16[512,1024]{1,0:T(8,128)(2,1)} %copy-done, f32[2,1024]{1,0:T(2,128)} %refs_3_.3, ...), custom_call_target="tpu_custom_call", output_to_operand_aliasing={{0}: (9, {}), {1}: (10, {})} | custom-call | tf_op jit(solution)/shard_map/attend1/pallas_call | solution.py:195
  100.4 0.0 copy-start.1
  100.5 1.2 copy-done.1
  101.7 0.0 copy-start.5
  101.7 0.9 copy-done.5
  102.6 20.8 %combine1.1 = bf16[512,1024]{1,0:T(8,128)(2,1)S(1)} custom-call(bf16[512,1024]{1,0:T(8,128)(2,1)S(1)} %copy-done.1, f32[512,128]{1,0:T(8,128)S(1)} %copy-done.5, f32[2,1024]{1,0:T(2,128)S(1)} %copy-done.7, f32[2,1024]{1,0:T(2,128)S(1)} %copy-done.8, bf16[2,128,1024]{2,1,0:T(8,128)(2,1)S(1)} %copy-done.4, bf16[2,1024,512]{2,1,0:T(8,128)(2,1)S(1)} %copy-done.2, ...), custom_call_target="tpu_custom_call" | custom-call | tf_op jit(solution)/shard_map/combine1/pallas_call | solution.py:328
  123.4 1.0 copy.24
Async XLA Ops:
  0.6 37.2 %copy-start.2 = (bf16[2,1024,512]{2,1,0:T(8,128)(2,1)S(1)}, bf16[2,1024,512]{2,1,0:T(8,128)(2,1)}, u32[]{:S(2)}) copy-start(bf16[2,1024,512]{2,1,0:T(8,128)(2,1)} %w_up_any.3) | copy-start | bytes 6291460
  0.6 37.2 %copy-start.3 = (bf16[512,1024]{1,0:T(8,128)(2,1)S(1)}, bf16[512,1024]{1,0:T(8,128)(2,1)}, u32[]{:S(2)}) copy-start(bf16[512,1024]{1,0:T(8,128)(2,1)} %hid_ref.1) | copy-start | bytes 3145732
  0.7 37.2 %copy-start.4 = (bf16[2,128,1024]{2,1,0:T(8,128)(2,1)S(1)}, bf16[2,128,1024]{2,1,0:T(8,128)(2,1)}, u32[]{:S(2)}) copy-start(bf16[2,128,1024]{2,1,0:T(8,128)(2,1)} %w_out_any.3) | copy-start | bytes 1572868
  0.7 37.2 %copy-start.7 = (f32[2,1024]{1,0:T(2,128)S(1)}, f32[2,1024]{1,0:T(2,128)}, u32[]{:S(2)}) copy-start(f32[2,1024]{1,0:T(2,128)} %gain_ref.3) | copy-start | bytes 24580
  0.7 37.2 %copy-start.8 = (f32[2,1024]{1,0:T(2,128)S(1)}, f32[2,1024]{1,0:T(2,128)}, u32[]{:S(2)}) copy-start(f32[2,1024]{1,0:T(2,128)} %bias_ref.3) | copy-start | bytes 24580
  0.7 37.2 %copy-start.9 = (bf16[2,1024]{1,0:T(2,128)(2,1)S(1)}, bf16[2,1024]{1,0:T(2,128)(2,1)}, u32[]{:S(2)}) copy-start(bf16[2,1024]{1,0:T(2,128)(2,1)} %b_out_ref.3) | copy-start | bytes 12292
  0.7 37.2 %copy-start.10 = (bf16[2,1024]{1,0:T(2,128)(2,1)S(1)}, bf16[2,1024]{1,0:T(2,128)(2,1)}, u32[]{:S(2)}) copy-start(bf16[2,1024]{1,0:T(2,128)(2,1)} %b_down_ref.3) | copy-start | bytes 12292
  0.7 37.2 %copy-start.11 = (bf16[2,512]{1,0:T(2,128)(2,1)S(1)}, bf16[2,512]{1,0:T(2,128)(2,1)}, u32[]{:S(2)}) copy-start(bf16[2,512]{1,0:T(2,128)(2,1)} %b_up_ref.3) | copy-start | bytes 6148
  37.9 1.0 copy-start.6
  62.8 1.0 copy-start
  100.4 1.2 copy-start.1
  101.7 0.9 copy-start.5

commit v3 on v2

--- a/solution.py
+++ b/solution.py
@@ -14,8 +14,9 @@
 MESH = pl.DeviceIdType.MESH
 LANES = 128
 BLOCK = 32
-SLOTS = 8
-AHEAD = 5
+SLOTS = 12
+AHEAD = 8
+GROUP = 16
 CHUNK = 128
 
 
@@ -56,11 +57,11 @@
 
 
 def attend_kernel(layer, num_rows, head, *refs):
-    (pos_ref, pos_sm, hid_any, gain_ref, bias_ref, w_any, b_ref, k_in, v_in) = refs[:9]
+    (pos_ref, pos_sm, hid_s, gain_ref, bias_ref, w_ref, b_ref, k_in, v_in) = refs[:9]
     refs = refs[9:]
     if layer > 0:
         refs = refs[2:]
-    (k_out, v_out, ctx_ref, hid_s, w_s, q_s, pos_s, kn_s, vn_s, k_buf, v_buf, rd_sem, wr_sem, in_sem) = refs
+    (k_out, v_out, ctx_ref, q_s, pos_s, kn_s, vn_s, k_buf, v_buf, rd_sem, wr_sem) = refs
     num_blocks = num_rows // BLOCK
     per_chunk = CHUNK // BLOCK
 
@@ -74,15 +75,9 @@
         return (pltpu.make_async_copy(k_buf.at[slot], k_out.at[layer, rows], wr_sem.at[0, slot]),
                 pltpu.make_async_copy(v_buf.at[slot], v_out.at[layer, rows], wr_sem.at[1, slot]))
 
-    hid_copy = pltpu.make_async_copy(hid_any, hid_s, in_sem.at[0])
-    w_copy = pltpu.make_async_copy(w_any.at[layer], w_s, in_sem.at[1])
-    hid_copy.start()
-    w_copy.start()
     for blk in range(SLOTS):
         for copy in reads(blk, blk):
-            copy.start()
-    hid_copy.wait()
-    w_copy.wait()
+            copy.start(priority=1)
 
     lane = iota((CHUNK, LANES), 1)
     low = lane < head
@@ -94,7 +89,7 @@
         pos_s[rows, :] = pos
         normed = normalize(hid_s[rows, :].astype(F32))
         attn_in = (normed * gain_ref[layer:layer + 1, :] + bias_ref[layer:layer + 1, :]).astype(BF)
-        qkv = jnp.dot(attn_in, w_s[...], preferred_element_type=F32) + b_ref[layer:layer + 1, :].astype(F32)
+        qkv = jnp.dot(attn_in, w_ref[layer], preferred_element_type=F32) + b_ref[layer:layer + 1, :].astype(F32)
         qkv = qkv.astype(BF).astype(F32)
         one, two, three = qkv[:, :LANES], qkv[:, LANES:2 * LANES], qkv[:, 2 * LANES:]
         query = jnp.where(low, one, two)
@@ -103,26 +98,41 @@
         q_s[rows, :] = rotate(query, tables, head // 8).astype(BF).astype(F32)
         key_t = jnp.transpose(rotate(key, tables, head // 8).astype(BF).astype(F32))
         val_t = jnp.transpose(value)
-        for i in range(per_chunk):
-            kn_s[c * per_chunk + i] = (pltpu.roll(key_t, (LANES - i * BLOCK) % LANES, 1) if i else key_t).astype(kn_s.dtype)
-            vn_s[c * per_chunk + i] = (pltpu.roll(val_t, (LANES - i * BLOCK) % LANES, 1) if i else val_t).astype(vn_s.dtype)
+        for i in range(CHUNK // GROUP):
+            kn_s[c * (CHUNK // GROUP) + i] = (pltpu.roll(key_t, LANES - i * GROUP, 1) if i else key_t).astype(kn_s.dtype)
+            vn_s[c * (CHUNK // GROUP) + i] = (pltpu.roll(val_t, LANES - i * GROUP, 1) if i else val_t).astype(vn_s.dtype)
 
     scale = head ** -0.5
     sub16 = iota((16, LANES), 0) % 8
     lane16 = iota((16, LANES), 1)
+    row16 = iota((16, LANES), 0)
     lane8 = iota((8, LANES), 1)
     even = (sub16 % 2) == 0
     first = sub16 < 4
     upper = (sub16 % 4) < 2
 
-    def merged(buf, new_s, slot, blk, j, hit):
-        shift = lax.rem(pos_sm[blk * BLOCK + j] + (LANES - j), LANES)
-        col = pltpu.roll(new_s[blk], shift, 1).astype(BF)
-        out = jnp.where(hit, col, buf[slot, j])
+    def merged(buf, cols, slot, j, hit):
+        out = jnp.where(hit, cols[:, j % 2 * LANES:(j % 2 + 1) * LANES], buf[slot, j])
         buf[slot, j] = out
         return out
 
-    def square(tiles):
+    def pair_cols(new_s, blk, j, p8):
+        tile = new_s[blk * (BLOCK // GROUP) + j // GROUP]
+        if layer == 0:
+            hot = [jnp.where((row16 == (j + i) % GROUP) & (lane16 == p8[(j + i) % 8:(j + i) % 8 + 1, :].astype(jnp.int32)), 1.0, 0.0) for i in range(2)]
+            hot = jnp.concatenate(hot, 1).astype(BF)
+            return jnp.dot(tile[:, :GROUP].astype(BF), hot, preferred_element_type=F32).astype(BF)
+        cols = []
+        for i in range(2):
+            shift = lax.rem(pos_sm[blk * BLOCK + j + i] + (LANES - (j + i) % GROUP), LANES)
+            cols.append(pltpu.roll(tile, shift, 1).astype(BF))
+        return jnp.concatenate(cols, 1)
+
+    def quad(buf, new_s, slot, blk, j, hits, p8):
+        tiles = []
+        for i in (0, 2):
+            cols = pair_cols(new_s, blk, j + i, p8)
+            tiles += [merged(buf, cols, slot, j + i, hits[i]), merged(buf, cols, slot, j + i + 1, hits[i + 1])]
         return jnp.concatenate([jnp.concatenate(tiles[:2], 1), jnp.concatenate(tiles[2:], 1)], 0)
 
     @pl.loop(0, num_blocks)
@@ -136,7 +146,7 @@
             for copy in writes(ahead - SLOTS, ahead_slot):
                 copy.wait()
             for copy in reads(ahead, ahead_slot):
-                copy.start()
+                copy.start(priority=1)
 
         for copy in reads(blk, slot):
             copy.wait()
@@ -151,7 +161,7 @@
             p16 = jnp.concatenate([p8, p8], 0)
             scores = []
             for t in range(2):
-                keys = square([merged(k_buf, kn_s, slot, blk, 8 * g + 4 * t + i, hits[4 * t + i]) for i in range(4)])
+                keys = quad(k_buf, kn_s, slot, blk, 8 * g + 4 * t, hits[4 * t:4 * t + 4], p8)
                 mine = first if t == 0 else ~first
                 lhs = jnp.concatenate([jnp.where(mine & upper, q16, 0.0), jnp.where(mine & ~upper, q16, 0.0)], 1).astype(BF)
                 out = jnp.dot(lhs, keys, preferred_element_type=F32)
@@ -163,7 +173,7 @@
             lhs = jnp.concatenate([jnp.where(even, prob, 0.0), jnp.where(even, 0.0, prob)], 1).astype(BF)
             ctx = []
             for t in range(2):
-                vals = square([merged(v_buf, vn_s, slot, blk, 8 * g + 4 * t + i, hits[4 * t + i]) for i in range(4)])
+                vals = quad(v_buf, vn_s, slot, blk, 8 * g + 4 * t, hits[4 * t:4 * t + 4], p8)
                 out = lax.dot_general(lhs, vals, (((1,), (1,)), ((), ())), preferred_element_type=F32)
                 ctx.append(jnp.where(upper, out[:, :LANES], out[:, LANES:]))
             c16 = jnp.where(first, ctx[0], ctx[1])
@@ -185,7 +195,7 @@
     vmem = pl.BlockSpec(memory_space=pltpu.VMEM)
     anyspace = pl.BlockSpec(memory_space=pl.ANY)
     operands = [positions, positions.reshape(-1), hidden, gain, bias, w_qkv, b_qkv, k_cache, v_cache]
-    specs = [vmem, pl.BlockSpec(memory_space=pltpu.SMEM), anyspace, vmem, vmem, anyspace, vmem, anyspace, anyspace]
+    specs = [vmem, pl.BlockSpec(memory_space=pltpu.SMEM), vmem, vmem, vmem, vmem, vmem, anyspace, anyspace]
     aliases = {}
     if prev is not None:
         operands += list(prev)
@@ -198,26 +208,23 @@
         in_specs=specs,
         out_specs=(anyspace, anyspace, vmem),
         scratch_shapes=[
-            pltpu.VMEM((num_rows, width), BF),
-            pltpu.VMEM(w_qkv.shape[1:], BF),
             pltpu.VMEM((num_rows, LANES), F32),
             pltpu.VMEM((num_rows, LANES), F32),
-            pltpu.VMEM((num_blocks, LANES, LANES), F32),
-            pltpu.VMEM((num_blocks, LANES, LANES), F32),
+            pltpu.VMEM((num_rows // GROUP, LANES, LANES), F32 if layer else BF),
+            pltpu.VMEM((num_rows // GROUP, LANES, LANES), F32 if layer else BF),
             pltpu.VMEM((SLOTS, BLOCK, inner, slots), BF),
             pltpu.VMEM((SLOTS, BLOCK, inner, slots), BF),
             pltpu.SemaphoreType.DMA((2, SLOTS)),
             pltpu.SemaphoreType.DMA((2, SLOTS)),
-            pltpu.SemaphoreType.DMA((2,)),
         ],
         input_output_aliases=aliases,
-        compiler_params=pltpu.CompilerParams(vmem_limit_bytes=56 * 1024 * 1024),
+        compiler_params=pltpu.CompilerParams(vmem_limit_bytes=44 * 1024 * 1024),
         name=f"attend{layer}",
     )(*operands)
 
 
-def combine_kernel(layer, num_rows, hid_ref, ctx_ref, gain_ref, bias_ref, w_out_any, w_up_any, b_up_ref, w_down_any, b_out_ref, b_down_ref,
-                   out_ref, w_out, w_up, w_down, part, half, pair_in, quad_in, final, in_sem,
+def combine_kernel(layer, num_rows, hid_ref, ctx_ref, gain_ref, bias_ref, w_out, w_up, b_up_ref, w_down, b_out_ref, b_down_ref,
+                   out_ref, part, half, pair_in, quad_in, final,
                    pair_send, pair_recv, quad_send, quad_recv, gather_send, gather_recv, fwd_send, fwd_recv):
     me = lax.axis_index("tp")
     core = lax.rem(me, 2)
@@ -234,11 +241,6 @@
     half_rows = CHUNK // 2
     piece = CHUNK // 8
 
-    weights = [pltpu.make_async_copy(src.at[layer], dst, in_sem.at[i])
-               for i, (src, dst) in enumerate([(w_up_any, w_up), (w_down_any, w_down), (w_out_any, w_out)])]
-    for copy in weights:
-        copy.start()
-
     barrier = pltpu.get_barrier_semaphore()
     peers = [partner] + [2 * o + core for o in others]
     for peer in peers:
@@ -271,10 +273,10 @@
         rows = pl.ds(c * CHUNK, CHUNK)
         normed = normalize(hid_ref[rows, :].astype(F32))
         mlp_in = (normed * gain_ref[layer:layer + 1, :] + bias_ref[layer:layer + 1, :]).astype(BF)
-        up = jnp.dot(mlp_in, w_up[...], preferred_element_type=F32) + b_up_ref[layer:layer + 1, :].astype(F32)
+        up = jnp.dot(mlp_in, w_up[layer], preferred_element_type=F32) + b_up_ref[layer:layer + 1, :].astype(F32)
         act = (0.5 * up * (1.0 + lax.erf(up * np.float32(np.sqrt(0.5))))).astype(BF)
-        total = jnp.dot(act, w_down[...], preferred_element_type=F32)
-        total = total + jnp.dot(ctx_ref[rows, :].astype(BF), w_out[...], preferred_element_type=F32)
+        total = jnp.dot(act, w_down[layer], preferred_element_type=F32)
+        total = total + jnp.dot(ctx_ref[rows, :].astype(BF), w_out[layer], preferred_element_type=F32)
         part[c] = total.astype(BF)
 
     def pair_done(c):
@@ -293,8 +295,6 @@
         total = total + b_out_ref[layer:layer + 1, :].astype(F32) + b_down_ref[layer:layer + 1, :].astype(F32)
         final[rows, :] = total.astype(BF)
 
-    for copy in weights:
-        copy.wait()
     for step in range(num_chunks + 4):
         if step < num_chunks:
             compute(step)
@@ -323,29 +323,24 @@
     num_rows, width = hidden.shape
     num_chunks = num_rows // CHUNK
     vmem = pl.BlockSpec(memory_space=pltpu.VMEM)
-    anyspace = pl.BlockSpec(memory_space=pl.ANY)
     dma = pltpu.SemaphoreType.DMA
     return pl.pallas_call(
         functools.partial(combine_kernel, layer, num_rows),
         out_shape=jax.ShapeDtypeStruct((num_rows, width), BF),
-        in_specs=[vmem, vmem, vmem, vmem, anyspace, anyspace, vmem, anyspace, vmem, vmem],
+        in_specs=[vmem] * 10,
         out_specs=vmem,
         scratch_shapes=[
-            pltpu.VMEM(w_out.shape[1:], BF),
-            pltpu.VMEM(w_up.shape[1:], BF),
-            pltpu.VMEM(w_down.shape[1:], BF),
             pltpu.VMEM((num_chunks, CHUNK, width), BF),
             pltpu.VMEM((num_chunks, CHUNK // 2, width), BF),
             pltpu.VMEM((num_chunks, CHUNK // 2, width), BF),
             pltpu.VMEM((num_chunks, 3, CHUNK // 8, width), BF),
             pltpu.VMEM((num_rows, width), BF),
-            dma((3,)),
             dma((num_chunks,)), dma((num_chunks,)),
             dma((num_chunks, 3)), dma((num_chunks, 3)),
             dma((num_chunks, 3)), dma((num_chunks, 3)),
             dma((num_chunks,)), dma((num_chunks,)),
         ],
-        compiler_params=pltpu.CompilerParams(collective_id=layer, has_side_effects=True, vmem_limit_bytes=48 * 1024 * 1024),
+        compiler_params=pltpu.CompilerParams(collective_id=layer, has_side_effects=True, vmem_limit_bytes=20 * 1024 * 1024),
         name=f"combine{layer}",
     )(hidden, ctx, gain, bias, w_out, w_up, b_up, w_down, b_out, b_down)
 

time: 125 us -> 126 us (level)
  local copies, waits for them, and re-layouts: 5.09 us -> 6.39 us
    unnamed x25 -> x33, local copies, waits for them, and re-layouts: 5.09 us -> 6.39 us
where the time goes in v3:
time: 126 us
  Pallas kernels  119 us (94%)
  local copies, waits for them, and re-layouts  6.39 us (5%)
    pallas_call x2, Pallas kernels, attend(): pl.pallas_call(functools.partial(attend_kernel, layer, num_rows, head), o...  74.8 us
    pallas_call x2, Pallas kernels, combine(): pl.pallas_call(functools.partial(combine_kernel, layer, num_rows), out_sh...  43.7 us
    unnamed x33, local copies, waits for them, and re-layouts  6.39 us

profile of v3, /device:TPU:0, one launch (start us, length us, event | category | flops | bytes accessed | tf_op | source)
XLA Modules:
  0.0 125.7 jit_solution(10062101593981921416)
XLA Ops:
  0.6 0.0 copy-start.2
  0.6 1.4 %copy-done.2 = bf16[2,1024,384]{2,1,0:T(8,128)(2,1)S(1)} copy-done((bf16[2,1024,384]{2,1,0:T(8,128)(2,1)S(1)}, bf16[2,1024,384]{2,1,0:T(8,128)(2,1)}, u32[]{:S(2)}) %copy-start.2) | copy-done | bytes 1572888
  2.0 0.0 copy-start.4
  2.0 1.2 copy-done.4
  3.3 0.0 copy-start.6
  3.3 0.7 copy-done.6
  4.0 0.0 copy-start.7
  4.0 0.7 copy-done.7
  4.7 0.0 copy-start.8
  4.7 0.7 copy-done.8
  5.3 0.0 copy-start.14
  5.3 0.7 copy-done.14
  6.0 0.0 copy-start
  6.0 0.0 copy-start.1
  6.0 0.0 copy-start.5
  6.0 0.0 copy-start.9
  6.0 0.0 copy-start.10
  6.0 0.0 copy-start.11
  6.1 0.0 copy-start.12
  6.1 0.0 copy-start.13
  6.1 0.0 copy-start.3
  6.1 0.0 copy-start.15
  6.1 44.7 %attend0.1 = (bf16[2,512,128,128]{3,2,1,0:T(8,128)(2,1)}, bf16[2,512,128,128]{3,2,1,0:T(8,128)(2,1)}, f32[512,128]{1,0:T(8,128)S(1)}) custom-call(s32[4,128]{1,0:T(4,128)S(1)} %bitcast.13, s32[512]{0:T(512)S(1)} %copy-done.6, bf16[512,1024]{1,0:T(8,128)(2,1)S(1)} %copy-done.4, f32[2,1024]{1,0:T(2,128)S(1)} %copy-done.7, f32[2,1024]{1,0:T(2,128)S(1)} %copy-done.8, ...), custom_call_target="tpu_custom_call" | custom-call | tf_op jit(solution)/shard_map/attend0/pallas_call | solution.py:205
  50.9 0.0 copy-done
  50.9 0.0 copy-done.1
  50.9 0.0 copy-done.5
  50.9 0.0 copy-done.9
  50.9 0.0 copy-done.10
  50.9 0.0 copy-done.11
  50.9 0.0 copy-done.12
  50.9 0.0 copy-done.13
  50.9 23.3 %combine0.1.refs_2_.hid_ref = bf16[512,1024]{1,0:T(8,128)(2,1)S(1)} custom-call(bf16[512,1024]{1,0:T(8,128)(2,1)S(1)} %copy-done.4, f32[512,128]{1,0:T(8,128)S(1)} %get-tuple-element.9.ctx_ref, f32[2,1024]{1,0:T(2,128)S(1)} %copy-done.9, f32[2,1024]{1,0:T(2,128)S(1)} %copy-done.10, bf16[2,128,1024]{2,1,0:T(8,128)(2,1)S(1)} %copy-done.5, ...), custom_call_target="tpu_custom_call" | custom-call | tf_op jit(solution)/shard_map/combine0/pallas_call | solution.py:327
  74.2 0.0 copy-done.3
  74.2 0.0 copy-done.15
  74.2 30.0 %attend1.1 = (bf16[2,512,128,128]{3,2,1,0:T(8,128)(2,1)}, bf16[2,512,128,128]{3,2,1,0:T(8,128)(2,1)}, f32[512,128]{1,0:T(8,128)S(1)}) custom-call(s32[4,128]{1,0:T(4,128)S(1)} %bitcast.14, s32[512]{0:T(512)S(1)} %copy-done.6, bf16[512,1024]{1,0:T(8,128)(2,1)S(1)} %combine0.1.refs_2_.hid_ref, ...), custom_call_target="tpu_custom_call", output_to_operand_aliasing={{0}: (9, {}), {1}: (10, {})} | custom-call | tf_op jit(solution)/shard_map/attend1/pallas_call | solution.py:205
  104.3 20.5 %combine1.1 = bf16[512,1024]{1,0:T(8,128)(2,1)S(1)} custom-call(bf16[512,1024]{1,0:T(8,128)(2,1)S(1)} %combine0.1.refs_2_.hid_ref, f32[512,128]{1,0:T(8,128)S(1)} %get-tuple-element.12.ctx_ref, f32[2,1024]{1,0:T(2,128)S(1)} %copy-done.9, f32[2,1024]{1,0:T(2,128)S(1)} %copy-done.10, bf16[2,128,1024]{2,1,0:T(8,128)(2,1)S(1)} %copy-done.5, ...), custom_call_target="tpu_custom_call" | custom-call | tf_op jit(solution)/shard_map/combine1/pallas_call | solution.py:327
  124.8 1.0 copy.24
Async XLA Ops:
  0.6 1.4 %copy-start.2 = (bf16[2,1024,384]{2,1,0:T(8,128)(2,1)S(1)}, bf16[2,1024,384]{2,1,0:T(8,128)(2,1)}, u32[]{:S(2)}) copy-start(bf16[2,1024,384]{2,1,0:T(8,128)(2,1)} %refs_5_.3) | copy-start | bytes 4718596
  2.0 1.2 copy-start.4
  3.3 0.7 copy-start.6
  4.0 0.7 copy-start.7
  4.7 0.7 copy-start.8
  5.3 0.7 copy-start.14
  6.0 44.8 %copy-start = (bf16[2,1024,512]{2,1,0:T(8,128)(2,1)S(1)}, bf16[2,1024,512]{2,1,0:T(8,128)(2,1)}, u32[]{:S(2)}) copy-start(bf16[2,1024,512]{2,1,0:T(8,128)(2,1)} %w_up.3) | copy-start | bytes 6291460
  6.0 44.8 %copy-start.1 = (bf16[2,512,1024]{2,1,0:T(8,128)(2,1)S(1)}, bf16[2,512,1024]{2,1,0:T(8,128)(2,1)}, u32[]{:S(2)}) copy-start(bf16[2,512,1024]{2,1,0:T(8,128)(2,1)} %w_down.3) | copy-start | bytes 6291460
  6.0 44.8 %copy-start.5 = (bf16[2,128,1024]{2,1,0:T(8,128)(2,1)S(1)}, bf16[2,128,1024]{2,1,0:T(8,128)(2,1)}, u32[]{:S(2)}) copy-start(bf16[2,128,1024]{2,1,0:T(8,128)(2,1)} %w_out.3) | copy-start | bytes 1572868
  6.0 44.9 %copy-start.9 = (f32[2,1024]{1,0:T(2,128)S(1)}, f32[2,1024]{1,0:T(2,128)}, u32[]{:S(2)}) copy-start(f32[2,1024]{1,0:T(2,128)} %gain_ref.3) | copy-start | bytes 24580
  6.0 44.9 %copy-start.10 = (f32[2,1024]{1,0:T(2,128)S(1)}, f32[2,1024]{1,0:T(2,128)}, u32[]{:S(2)}) copy-start(f32[2,1024]{1,0:T(2,128)} %bias_ref.3) | copy-start | bytes 24580
  6.0 44.9 %copy-start.11 = (bf16[2,1024]{1,0:T(2,128)(2,1)S(1)}, bf16[2,1024]{1,0:T(2,128)(2,1)}, u32[]{:S(2)}) copy-start(bf16[2,1024]{1,0:T(2,128)(2,1)} %b_out_ref.3) | copy-start | bytes 12292
  6.1 44.9 %copy-start.12 = (bf16[2,1024]{1,0:T(2,128)(2,1)S(1)}, bf16[2,1024]{1,0:T(2,128)(2,1)}, u32[]{:S(2)}) copy-start(bf16[2,1024]{1,0:T(2,128)(2,1)} %b_down_ref.3) | copy-start | bytes 12292
  6.1 44.9 %copy-start.13 = (bf16[2,512]{1,0:T(2,128)(2,1)S(1)}, bf16[2,512]{1,0:T(2,128)(2,1)}, u32[]{:S(2)}) copy-start(bf16[2,512]{1,0:T(2,128)(2,1)} %b_up_ref.3) | copy-start | bytes 6148
  6.1 68.1 %copy-start.3 = (bf16[2,1024,384]{2,1,0:T(8,128)(2,1)S(1)}, bf16[2,1024,384]{2,1,0:T(8,128)(2,1)}, u32[]{:S(2)}) copy-start(bf16[2,1024,384]{2,1,0:T(8,128)(2,1)} %refs_5_.3) | copy-start | bytes 4718596
  6.1 68.1 %copy-start.15 = (bf16[2,384]{1,0:T(2,128)(2,1)S(1)}, bf16[2,384]{1,0:T(2,128)(2,1)}, u32[]{:S(2)}) copy-start(bf16[2,384]{1,0:T(2,128)(2,1)} %refs_6_.3) | copy-start | bytes 4612
